TPU v7x, 32 devices: a whole 2x2x4 slice. The times are simulated.
32 devices in a mesh: row: 4 (over y, x), col: 8 (over z, core).
Axes of the slice: x: 2, y: 2, z: 4, core: 2. Of those that a mesh axis runs over, the one named last changes fastest.
Arguments:
- features: float32 [8, 1536, 256], P('col', 'row'), may hold values from -1000 to 1000
- tiles: bfloat16 [8, 4, 8, 9, 128, 128], P('col', 'row'), may hold values from -0.1875 to 0.1875
- tile_ids: int32 [8, 4, 8, 9], P('col', 'row'), may hold values from 0 to 35
- tile_counts: int32 [8, 4, 8], P('col', 'row'), may hold values from 1 to 9, as said below
Outputs:
- propagated: float32 [8, 1536, 256], P('col', 'row')
- residual_norms: float32 [3], replicated
Inputs may be any that keep to these rules, and one draw needn't show every extreme that they name: `tile_ids`: each id is a row tile times 3 plus a column tile; ids may repeat within a list. `tile_counts`: slots at or after the count hold values to be ignored; in every draw some device has 9 live slots for some source block.
All inputs are finite; a program needn't handle non-finite values.
Results may differ from a plain program's by a relative error of at most 0.014.
Values may be sent and summed in bfloat16 or wider, within the bound.
A program may use at most 64 MiB of HBM per device.

v0:
```python
import jax
import jax.numpy as jnp
from jax import lax
from jax.sharding import PartitionSpec as P

ITERS = 3


ALPHA = 0.1


def source_term(running, source_block, matrices, slot_ids, live_count):
    tile_size = matrices.shape[-1]
    slot_count = slot_ids.shape[0]
    row_tiles = running.shape[0]
    columns = source_block.shape[-1]
    col_tiles = source_block.shape[0] // tile_size
    pieces = source_block.reshape(col_tiles, tile_size, columns)
    picked = jnp.take(pieces, slot_ids % col_tiles, axis=0)
    products = jnp.einsum("sij,sjf->sif", matrices, picked, preferred_element_type=jnp.float32)
    in_use = lax.iota(jnp.int32, slot_count) < live_count
    placement = (
        (slot_ids // col_tiles)[None, :] == lax.iota(jnp.int32, row_tiles)[:, None]
    ) & in_use[None, :]
    chooser = placement.astype(jnp.bfloat16)
    high_part = products.astype(jnp.bfloat16)
    low_part = (products - high_part.astype(jnp.float32)).astype(jnp.bfloat16)
    placed = jnp.einsum("rs,sif->rif", chooser, high_part, preferred_element_type=jnp.float32)
    placed = placed + jnp.einsum(
        "rs,sif->rif", chooser, low_part, preferred_element_type=jnp.float32
    )
    return running + placed


def accumulate(running, blocks, my_tiles, my_ids, my_counts):

    def sweep(carried, element):
        source_block, offset = element
        matrices = lax.dynamic_index_in_dim(my_tiles, offset, 0, keepdims=False)
        slot_ids = lax.dynamic_index_in_dim(my_ids, offset, 0, keepdims=False)
        live_count = lax.dynamic_index_in_dim(my_counts, offset, 0, keepdims=False)
        return (source_term(carried, source_block, matrices, slot_ids, live_count), None)

    offsets = jnp.arange(blocks.shape[0], dtype=jnp.int32)
    running, _ = lax.scan(sweep, running, (blocks, offsets))
    return running


def local(features, tiles, tile_ids, tile_counts):
    teleport = features[0]
    my_tiles = tiles[0, 0]
    my_ids = tile_ids[0, 0]
    my_counts = tile_counts[0, 0]
    tile_size = my_tiles.shape[-1]
    columns = teleport.shape[-1]
    row_tiles = lax.axis_size("row") * teleport.shape[0] // tile_size
    total_count = teleport.shape[0] * lax.axis_size("row") * lax.axis_size("col") * columns
    current = teleport
    squares = []
    for iteration in range(ITERS):
        rounded = current.astype(jnp.bfloat16)[None]
        zeroed = jnp.zeros((row_tiles, tile_size, columns), jnp.float32)
        partial_value = accumulate(
            zeroed, lax.all_gather(rounded, "col", axis=0, tiled=True), my_tiles, my_ids, my_counts
        )
        partial_value = partial_value.reshape(row_tiles * tile_size, columns)
        summed = lax.psum_scatter(partial_value, "row", scatter_dimension=0, tiled=True)
        updated = 0.9 * summed + ALPHA * teleport
        local_sum = jnp.sum((updated - current) ** 2)
        squares.append(local_sum)
        current = updated
    stacked = jnp.stack(squares)
    stacked = lax.psum(stacked, ("row", "col"))
    residual_norms = jnp.sqrt(stacked / total_count)
    return (current[None], residual_norms)


def solution(mesh):
    in_specs = (
        P("col", "row", None),
        P("col", "row", None, None, None, None),
        P("col", "row", None, None),
        P("col", "row", None),
    )
    out_specs = (P("col", "row", None), P())
    return jax.shard_map(local, mesh=mesh, in_specs=in_specs, out_specs=out_specs, check_vma=False)
```

profile of v0, /device:TPU:0, one launch (start us, length us, event | category | flops | bytes accessed | tf_op | source)
XLA Modules:
  0.0 510.6 jit_solution(9565376544211998079)
XLA Ops:
  7.2 1.7 convert_element_type.67
  9.0 29.2 %all-gather.6.cloned.1.call-done = bf16[8,384,256]{2,1,0:T(8,128)(2,1)} async-done(((bf16[1,384,256]{2,1,0:T(8,128)(2,1)}), bf16[8,384,256]{2,1,0:T(8,128)(2,1)}) %all-gather.6.cloned.1.call-update) | async-done | bytes 1572880 | tf_op jit(solution)/shard_map/all_gather | solution.py:64
  38.2 95.3 %while.39 = (s32[]{:T(128)}, f32[12,128,256]{2,0,1:T(8,128)}, s32[8]{0:T(128)S(1)}, s32[8,9]{1,0:T(8,128)}, s32[8]{0:T(128)}, /*index=5*/bf16[8,9,128,128]{3,2,1...) while((s32[]{:T(128)}, f32[12,128,256]{2,0,1:T(8,128)}, ...), condition=%wide.region_1.3_spmd.clone, body=%wide.region_0.2_spmd.clone.sunk | while | flops 92309104 | bytes 11113126 | solution.py:45
  43.0 1.3 subtract_convert_fusion.6
  46.8 1.9 select_add_fusion.6
  53.5 1.3 subtract_convert_fusion.6
  57.3 3.5 select_add_fusion.6
  65.6 1.3 subtract_convert_fusion.6
  69.4 3.5 select_add_fusion.6
  77.7 1.3 subtract_convert_fusion.6
  81.6 3.5 select_add_fusion.6
  89.9 1.3 subtract_convert_fusion.6
  93.7 3.5 select_add_fusion.6
  102.0 1.3 subtract_convert_fusion.6
  105.8 3.5 select_add_fusion.6
  114.1 1.3 subtract_convert_fusion.6
  117.9 3.5 select_add_fusion.6
  126.2 1.3 subtract_convert_fusion.6
  130.0 3.5 select_add_fusion.6
  133.5 3.7 copy.21
  137.3 30.4 %reduce-scatter.4.cloned.1.call-done = f32[384,256]{1,0:T(8,128)} async-done(((f32[1536,256]{1,0:T(8,128)}), f32[384,256]{1,0:T(8,128)}) %reduce-scatter.4.cloned.1.call-update) | async-done | bytes 393232 | tf_op jit(solution)/shard_map/reduce_scatter | solution.py:67
  167.7 1.7 fusion.63
  169.5 25.7 %all-gather.8.cloned.1.call-done = bf16[3072,256]{1,0:T(8,128)(2,1)} async-done(((bf16[384,256]{1,0:T(8,128)(2,1)}), bf16[3072,256]{1,0:T(8,128)(2,1)}) %all-gather.8.cloned.1.call-update) | async-done | bytes 1572880 | tf_op jit(solution)/shard_map/all_gather | solution.py:64
  195.2 84.2 %while.40 = (s32[]{:T(128)}, f32[12,128,256]{2,0,1:T(8,128)}, s32[8]{0:T(128)S(1)}, s32[8,9]{1,0:T(8,128)S(1)}, s32[8]{0:T(128)S(1)}, /*index=5*/bf16[8,9,128,12...) while((s32[]{:T(128)}, f32[12,128,256]{2,0,1:T(8,128)}, ...), condition=%wide.region_4.6_spmd.clone, body=%wide.region_3.5_spmd.clone.sunk | while | flops 92309104 | bytes 11112970 | solution.py:45
  199.3 1.3 subtract_convert_fusion.7
  202.4 1.9 select_add_fusion.7
  208.5 1.3 subtract_convert_fusion.7
  211.6 3.5 select_add_fusion.7
  219.2 1.3 subtract_convert_fusion.7
  222.3 3.5 select_add_fusion.7
  229.9 1.3 subtract_convert_fusion.7
  233.0 3.5 select_add_fusion.7
  240.6 1.3 subtract_convert_fusion.7
  243.8 3.5 select_add_fusion.7
  251.4 1.3 subtract_convert_fusion.7
  254.5 3.5 select_add_fusion.7
  262.1 1.3 subtract_convert_fusion.7
  265.2 3.5 select_add_fusion.7
  272.8 1.3 subtract_convert_fusion.7
  275.9 3.5 select_add_fusion.7
  279.5 3.7 copy.22
  283.2 30.4 %reduce-scatter.6.cloned.1.call-done = f32[384,256]{1,0:T(8,128)} async-done(((f32[1536,256]{1,0:T(8,128)}), f32[384,256]{1,0:T(8,128)}) %reduce-scatter.6.cloned.1.call-update) | async-done | bytes 393232 | tf_op jit(solution)/shard_map/reduce_scatter | solution.py:67
  313.6 1.7 fusion.64
  315.4 25.6 %all-gather.10.cloned.1.call-done = bf16[3072,256]{1,0:T(8,128)(2,1)} async-done(((bf16[384,256]{1,0:T(8,128)(2,1)}), bf16[3072,256]{1,0:T(8,128)(2,1)}) %all-gather.10.cloned.1.call-update) | async-done | bytes 1572880 | tf_op jit(solution)/shard_map/all_gather | solution.py:64
  340.9 84.2 %while.41 = (s32[]{:T(128)}, f32[12,128,256]{2,0,1:T(8,128)}, s32[8]{0:T(128)S(1)}, s32[8,9]{1,0:T(8,128)S(1)}, s32[8]{0:T(128)S(1)}, /*index=5*/bf16[8,9,128,12...) while((s32[]{:T(128)}, f32[12,128,256]{2,0,1:T(8,128)}, ...), condition=%wide.region_7.9_spmd.clone, body=%wide.region_6.8_spmd.clone.sunk | while | flops 92309104 | bytes 11112970 | solution.py:45
  345.1 1.3 subtract_convert_fusion.8
  348.2 1.9 select_add_fusion.8
  354.2 1.3 subtract_convert_fusion.8
  357.3 3.5 select_add_fusion.8
  364.9 1.3 subtract_convert_fusion.8
  368.0 3.5 select_add_fusion.8
  375.6 1.3 subtract_convert_fusion.8
  378.8 3.5 select_add_fusion.8
  386.4 1.3 subtract_convert_fusion.8
  389.5 3.5 select_add_fusion.8
  400.2 3.5 select_add_fusion.8
  407.8 1.3 subtract_convert_fusion.8
  410.9 3.5 select_add_fusion.8
  421.7 3.5 select_add_fusion.8
  425.2 3.7 copy.23
  429.0 30.4 %reduce-scatter.8.cloned.1.call-done = f32[384,256]{1,0:T(8,128)} async-done(((f32[1536,256]{1,0:T(8,128)}), f32[384,256]{1,0:T(8,128)}) %reduce-scatter.8.cloned.1.call-update) | async-done | bytes 393232 | tf_op jit(solution)/shard_map/reduce_scatter | solution.py:67
  459.4 2.6 fusion.61
  462.0 2.0 pad_maximum_fusion
  464.0 39.3 %psum.7 = f32[3]{0:T(128)S(1)} all-reduce(f32[3]{0:T(128)S(1)} %pad_maximum_fusion), channel_id=1, replica_groups=mesh['row'=4,'col'=8] {'row','col'}, use_global_device_ids=true, to_apply=%region_12.14 | all-reduce | flops 3 | bytes 24 | tf_op jit(solution)/shard_map/psum | solution.py:73
  (263 shorter events, 107.8 us)
Async XLA Ops:
  7.2 31.0 %all-gather.6.cloned.1.call-start = ((), (), s32[]{:S(2)}) async-start(), calls=%async_computation.3 | async-start | bytes 1769472 | tf_op jit(solution)/shard_map/all_gather | solution.py:64
  8.9 158.7 %reduce-scatter.4.cloned.1.call-start = ((), (), s32[]{:S(2)}) async-start(), calls=%async_computation.4 | async-start | bytes 1966080 | tf_op jit(solution)/shard_map/reduce_scatter | solution.py:67
  38.2 6.9 %copy-start.4 = (s32[8]{0:T(128)S(1)}, s32[8]{0:T(128)}, u32[]{:S(2)}) copy-start(s32[8]{0:T(128)} %get-tuple-element.589) | copy-start | bytes 100 | tf_op jit(solution)/shard_map/while
  48.7 6.9 %copy-start.4 = (s32[8]{0:T(128)S(1)}, s32[8]{0:T(128)}, u32[]{:S(2)}) copy-start(s32[8]{0:T(128)} %get-tuple-element.589) | copy-start | bytes 100 | tf_op jit(solution)/shard_map/while
  60.8 6.9 %copy-start.4 = (s32[8]{0:T(128)S(1)}, s32[8]{0:T(128)}, u32[]{:S(2)}) copy-start(s32[8]{0:T(128)} %get-tuple-element.589) | copy-start | bytes 100 | tf_op jit(solution)/shard_map/while
  73.0 6.9 %copy-start.4 = (s32[8]{0:T(128)S(1)}, s32[8]{0:T(128)}, u32[]{:S(2)}) copy-start(s32[8]{0:T(128)} %get-tuple-element.589) | copy-start | bytes 100 | tf_op jit(solution)/shard_map/while
  85.1 6.9 %copy-start.4 = (s32[8]{0:T(128)S(1)}, s32[8]{0:T(128)}, u32[]{:S(2)}) copy-start(s32[8]{0:T(128)} %get-tuple-element.589) | copy-start | bytes 100 | tf_op jit(solution)/shard_map/while
  97.2 6.9 %copy-start.4 = (s32[8]{0:T(128)S(1)}, s32[8]{0:T(128)}, u32[]{:S(2)}) copy-start(s32[8]{0:T(128)} %get-tuple-element.589) | copy-start | bytes 100 | tf_op jit(solution)/shard_map/while
  109.3 6.9 %copy-start.4 = (s32[8]{0:T(128)S(1)}, s32[8]{0:T(128)}, u32[]{:S(2)}) copy-start(s32[8]{0:T(128)} %get-tuple-element.589) | copy-start | bytes 100 | tf_op jit(solution)/shard_map/while
  121.4 6.9 %copy-start.4 = (s32[8]{0:T(128)S(1)}, s32[8]{0:T(128)}, u32[]{:S(2)}) copy-start(s32[8]{0:T(128)} %get-tuple-element.589) | copy-start | bytes 100 | tf_op jit(solution)/shard_map/while
  133.5 34.2 %copy-start = (f32[1,384,256]{2,1,0:T(8,128)S(1)}, f32[1,384,256]{2,1,0:T(8,128)}, u32[]{:S(2)}) copy-start(f32[1,384,256]{2,1,0:T(8,128)} %param.12) | copy-start | bytes 1179652
  137.2 58.0 %copy-start.3 = (s32[8,9]{1,0:T(8,128)S(1)}, s32[8,9]{1,0:T(8,128)}, u32[]{:S(2)}) copy-start(s32[8,9]{1,0:T(8,128)} %get-tuple-element.679) | copy-start | bytes 868
  137.2 58.0 %copy-start.5 = (s32[8]{0:T(128)S(1)}, s32[8]{0:T(128)}, u32[]{:S(2)}) copy-start(s32[8]{0:T(128)} %get-tuple-element.681) | copy-start | bytes 100
  137.3 57.9 %all-gather.8.cloned.1.call-start = ((), (), s32[]{:S(2)}) async-start(), calls=%async_computation.7 | async-start | bytes 1769472 | tf_op jit(solution)/shard_map/all_gather | solution.py:64
  169.4 144.1 %reduce-scatter.6.cloned.1.call-start = ((), (), s32[]{:S(2)}) async-start(), calls=%async_computation.5 | async-start | bytes 1966080 | tf_op jit(solution)/shard_map/reduce_scatter | solution.py:67
  283.2 57.8 %all-gather.10.cloned.1.call-start = ((), (), s32[]{:S(2)}) async-start(), calls=%async_computation.8 | async-start | bytes 1769472 | tf_op jit(solution)/shard_map/all_gather | solution.py:64
  315.3 144.1 %reduce-scatter.8.cloned.1.call-start = ((), (), s32[]{:S(2)}) async-start(), calls=%async_computation.6 | async-start | bytes 1966080 | tf_op jit(solution)/shard_map/reduce_scatter | solution.py:67
  425.2 34.2 %copy-start.1 = (f32[384,256]{1,0:T(8,128)S(1)}, f32[384,256]{1,0:T(8,128)}, u32[]{:S(2)}) copy-start(f32[384,256]{1,0:T(8,128)} %reduce-scatter.4.cloned.1.call-done) | copy-start | bytes 1179652
  425.2 34.2 %copy-start.2 = (f32[384,256]{1,0:T(8,128)S(1)}, f32[384,256]{1,0:T(8,128)}, u32[]{:S(2)}) copy-start(f32[384,256]{1,0:T(8,128)} %reduce-scatter.6.cloned.1.call-done) | copy-start | bytes 1179652
Sparse Core Ops, SparseCore 0:
  10.2 27.9 all-gather.5
  137.4 30.2 reduce-scatter.3
  169.9 25.2 all-gather.7
  283.3 30.2 reduce-scatter.5
  315.6 25.2 all-gather.9
  429.1 30.2 reduce-scatter.7
where the time goes:
time: 515 us; the launch traced here: 511 us
  waiting for transfers between devices  172 us (33%)
  matrix products  123 us (24%)
  local copies, waits for them, and re-layouts  76.1 us (15%)
  loops' own time  47.8 us (9%)
  blocking collectives  39.3 us (8%)
  other arithmetic  38 us (7%)
  between operations  14.1 us (3%)
    reduce_scatter x3, waiting for transfers between devices, local(): lax.psum_scatter(partial_value, 'row', scatter_dimension=0, tiled=True)  91.2 us
    all_gather x3, waiting for transfers between devices, local(): lax.all_gather(rounded, 'col', axis=0, tiled=True)  80.5 us
    dot_general x24, matrix products, source_term(): jnp.einsum('rs,sif->rif', chooser, low_part, preferred_element_type=jnp.f...  79.4 us
    another operation x3, loops' own time, accumulate(): running, _ = lax.scan(sweep, running, (blocks, offsets))  47.8 us
    psum x1, blocking collectives, local(): stacked = lax.psum(stacked, ('row', 'col'))  39.3 us
    dynamic_slice x48, local copies, waits for them, and re-layouts, accumulate(): running, _ = lax.scan(sweep, running, (blocks, offsets))  36.7 us
    dot_general x24, matrix products, source_term(): jnp.einsum('sij,sjf->sif', matrices, picked, preferred_element_type=jnp.f...  32.4 us
    lt x24, other arithmetic, source_term(): in_use = lax.iota(jnp.int32, slot_count) < live_count  15.6 us
  transfers between devices with their start and end apart: 6, of which 6 were waited for; matrix products, arithmetic and copies ran while one was open for 0% of the time, Pallas kernels for 0%

commit v1 on v0

v1 whole, which is shorter than its diff:
```python
import functools

import jax
import jax.numpy as jnp
from jax import lax
from jax.experimental import pallas as pl
from jax.experimental.pallas import tpu as pltpu
from jax.sharding import PartitionSpec as P

ITERS = 3
ALPHA = 0.1
CHUNKS = 2
MESH = pl.DeviceIdType.MESH


def kernel(
    nrow, ncol, prev_ref, last_ref, feat_ref, tiles_ref, out_ref, norm_ref,
    dense, buf0, buf1, gathered, acc, current, stage, landed, squares, sq_row, sq_col,
    tile_sem, ag_send, ag_recv, d2d_send, rs_send, rs_recv, sq_send_row, sq_recv_row, sq_send_col, sq_recv_col,
):
    nz = ncol // 2
    nodes, feats = feat_ref.shape
    slots = tiles_ref.shape[1]
    tile = tiles_ref.shape[-1]
    width = feats // CHUNKS
    row_tiles = nrow * nodes // tile
    col_tiles = nodes // tile
    r = lax.axis_index("row")
    c = lax.axis_index("col")
    z = c // 2
    core = c % 2
    sibling = z * 2 + 1 - core
    bufs = (buf0, buf1)

    def tile_copy(q, slot):
        return pltpu.make_async_copy(
            tiles_ref.at[pl.ds(2 * q, 2)], bufs[slot].at[:, pl.ds(0, slots)], tile_sem.at[slot]
        )

    for slot in range(2):
        tile_copy(slot, slot).start()

    barrier = pltpu.get_barrier_semaphore()
    for k in range(1, ncol):
        pl.semaphore_signal(barrier, inc=1, device_id={"col": (c + k) % ncol}, device_id_type=MESH)
    for k in range(1, nrow):
        pl.semaphore_signal(barrier, inc=1, device_id={"row": (r + k) % nrow}, device_id_type=MESH)
    for ch in range(CHUNKS):
        cols = slice(ch * width, (ch + 1) * width)
        gathered[0, ch, c] = feat_ref[:, cols].astype(jnp.bfloat16)
    pl.semaphore_wait(barrier, ncol - 1 + nrow - 1)

    def peer(k):
        if nz == 4:
            return (z, z + 1 - 2 * (z % 2), (z + 2) % 4, 3 - z)[k]
        return (z + k) % nz

    def block_copy(t, ch, source, target, send_sem):
        par = t % 2
        ref = gathered.at[par, ch, source]
        return pltpu.make_async_remote_copy(
            src_ref=ref, dst_ref=ref, send_sem=send_sem, recv_sem=ag_recv.at[par, ch, source],
            device_id={"col": target}, device_id_type=MESH,
        )

    far = [nz == 4 and k == 3 for k in range(nz)]

    def direct(k, act):
        if far[k]:
            pl.when((z == 1) | (z == 2))(act)
        else:
            act()

    send_order = [2, 1, 3] if nz == 4 else list(range(1, nz))

    def gather_send(t, ch):
        for k in send_order:
            def go(k=k):
                copy = block_copy(t, ch, c, peer(k) * 2 + core, ag_send.at[ch, k])
                if t > 0:
                    copy.wait_send()
                copy.start()
            direct(k, go)
        copy = block_copy(t, ch, c, sibling, d2d_send.at[ch, 0])
        if t > 0:
            copy.wait_send()
        copy.start()

    def gather_drain(ch):
        for k in send_order:
            def go(k=k):
                block_copy(0, ch, c, peer(k) * 2 + core, ag_send.at[ch, k]).wait_send()
            direct(k, go)
        for k in range(nz):
            block_copy(0, ch, c, sibling, d2d_send.at[ch, k]).wait_send()
        if nz == 4:
            @pl.when((z == 1) | (z == 2))
            def _():
                block_copy(0, ch, c, sibling, ag_send.at[ch, 0]).wait_send()

    def receive(t, ch, k):
        source = peer(k) * 2 + core
        block_copy(t, ch, source, sibling, d2d_send.at[ch, k]).wait_recv()
        if nz == 4 and k == 2:
            @pl.when((z == 1) | (z == 2))
            def _():
                copy = block_copy(t, ch, source, 6 * (z - 1) + core, ag_send.at[ch, 0])
                if t > 0:
                    copy.wait_send()
                copy.start()
        copy = block_copy(t, ch, source, sibling, d2d_send.at[ch, k])
        if t > 0:
            copy.wait_send()
        copy.start()

    def share_copy(t, ch, k):
        par = t % 2
        return pltpu.make_async_remote_copy(
            src_ref=stage.at[ch, k - 1], dst_ref=landed.at[par, ch, r],
            send_sem=rs_send.at[ch, k - 1], recv_sem=rs_recv.at[par, ch, r],
            device_id={"row": (r + k) % nrow}, device_id_type=MESH,
        )

    def product(t, ch, k):
        q = peer(k)
        par = t % 2
        other = q * 2 + 1 - core
        block_copy(t, ch, other, sibling, d2d_send.at[ch, 0]).wait_recv()
        source = gathered[par, ch, pl.ds(2 * q, 2)].reshape(2 * nodes, width)

        def part(j):
            return jnp.dot(dense[q, pl.ds(j * nodes, nodes)], source, preferred_element_type=jnp.float32)

        if k < nz - 1:
            def one(j, carry):
                rows = pl.ds(j * nodes, nodes)
                acc[ch, rows] = part(j) if k == 0 else acc[ch, rows] + part(j)
                return carry
            lax.fori_loop(0, nrow, one, 0)
            return
        for k2 in list(range(1, nrow)) + [0]:
            j = (r + k2) % nrow
            rows = pl.ds(j * nodes, nodes)
            total = acc[ch, rows] + part(j)
            if k2 == 0:
                acc[ch, rows] = total
                continue
            if t > 0:
                share_copy(t, ch, k2).wait_send()
            stage[ch, k2 - 1] = total.astype(jnp.bfloat16)
            share_copy(t, ch, k2).start()

    def update(t, ch):
        par = t % 2
        cols = slice(ch * width, (ch + 1) * width)
        summed = acc[ch, pl.ds(r * nodes, nodes)]
        for k in range(1, nrow):
            j = (r + k) % nrow
            pltpu.make_async_remote_copy(
                src_ref=stage.at[ch, 0], dst_ref=landed.at[par, ch, j], send_sem=rs_send.at[ch, 0],
                recv_sem=rs_recv.at[par, ch, j], device_id={"row": j}, device_id_type=MESH,
            ).wait_recv()
            summed = summed + landed[par, ch, j].astype(jnp.float32)
        teleport = feat_ref[:, cols]
        updated = (1.0 - ALPHA) * summed + ALPHA * teleport
        before = teleport if t == 0 else current[:, cols]
        if t < ITERS - 1:
            gathered[(t + 1) % 2, ch, c] = updated.astype(jnp.bfloat16)
            gather_send(t + 1, ch)
            current[:, cols] = updated
        else:
            out_ref[:, cols] = updated
        change = jnp.sum((updated - before) ** 2, axis=0, keepdims=True)
        squares[t : t + 1] = change if ch == 0 else squares[t : t + 1] + change

    for ch in range(CHUNKS):
        gather_send(0, ch)

    zero = jnp.zeros((tile, tile), jnp.bfloat16)
    for slot in range(2):
        for half in range(2):
            bufs[slot][half, slots] = zero

    def build(step, carry):
        for slot in range(2):
            q = step * 2 + slot
            buf = bufs[slot]
            tile_copy(q, slot).wait()
            for half in range(2):
                s = 2 * q + half
                for k in range(1, slots):
                    buf[half, k] = buf[half, k] + buf[half, prev_ref[s, k]]
                for i in range(row_tiles):
                    for j in range(col_tiles):
                        at = half * nodes + j * tile
                        dense[q, i * tile : (i + 1) * tile, at : at + tile] = buf[half, last_ref[s, i * col_tiles + j]]

            @pl.when(q + 2 < nz)
            def _():
                tile_copy(q + 2, slot).start()
        return carry

    squares[...] = jnp.zeros_like(squares)
    lax.fori_loop(0, nz // 2, build, 0)

    pending = None
    for t in range(ITERS):
        for ch in range(CHUNKS):
            for k in range(1, nz):
                receive(t, ch, k)
                if k == nz - 1 and pending is not None:
                    update(*pending)
                product(t, ch, k - 1)
            product(t, ch, nz - 1)
            pending = (t, ch)
    update(*pending)

    def sq_copy(axis, size, me, k, buffer, send, recv):
        return pltpu.make_async_remote_copy(
            src_ref=buffer.at[me], dst_ref=buffer.at[me], send_sem=send.at[k], recv_sem=recv.at[me],
            device_id={axis: (me + k) % size}, device_id_type=MESH,
        )

    total = squares[...]
    for axis, size, me, buffer, send, recv in (
        ("row", nrow, r, sq_row, sq_send_row, sq_recv_row),
        ("col", ncol, c, sq_col, sq_send_col, sq_recv_col),
    ):
        buffer[me] = total
        for k in range(1, size):
            sq_copy(axis, size, me, k, buffer, send, recv).start()
        for k in range(1, size):
            j = (me + k) % size
            pltpu.make_async_remote_copy(
                src_ref=buffer.at[me], dst_ref=buffer.at[j], send_sem=send.at[k], recv_sem=recv.at[j],
                device_id={axis: j}, device_id_type=MESH,
            ).wait_recv()
        total = buffer[0]
        for j in range(1, size):
            total = total + buffer[j]
        for k in range(1, size):
            sq_copy(axis, size, me, k, buffer, send, recv).wait_send()
    count = nrow * ncol * nodes * feats
    norms = jnp.sqrt(jnp.sum(total, axis=1, keepdims=True) / count)
    norm_ref[...] = jnp.broadcast_to(norms, norm_ref.shape)

    for ch in range(CHUNKS):
        gather_drain(ch)
        for k in range(1, nrow):
            share_copy(0, ch, k).wait_send()


def local(nrow, ncol, features, tiles, tile_ids, tile_counts):
    teleport = features[0]
    my_tiles = tiles[0, 0]
    my_ids = tile_ids[0, 0]
    my_counts = tile_counts[0, 0]
    nodes, feats = teleport.shape
    sources, slots, tile, _ = my_tiles.shape
    nz = ncol // 2
    width = feats // CHUNKS
    places = (nrow * nodes // tile) * (nodes // tile)
    slot = lax.iota(jnp.int32, slots)
    live = slot[None, :] < my_counts[:, None]
    same = (my_ids[:, :, None] == my_ids[:, None, :]) & live[:, None, :] & (slot[None, None, :] < slot[None, :, None])
    prev = jnp.max(jnp.where(same, slot[None, None, :], -1), axis=2)
    prev = jnp.where(prev < 0, slots, prev)
    here = (my_ids[:, None, :] == lax.iota(jnp.int32, places)[None, :, None]) & live[:, None, :]
    last = jnp.max(jnp.where(here, slot[None, None, :], -1), axis=2)
    last = jnp.where(last < 0, slots, last)
    bf16, f32 = jnp.bfloat16, jnp.float32
    vmem, smem = pltpu.VMEM, pltpu.SMEM
    dma = pltpu.SemaphoreType.DMA
    out, norms = pl.pallas_call(
        functools.partial(kernel, nrow, ncol),
        out_shape=(jax.ShapeDtypeStruct((nodes, feats), f32), jax.ShapeDtypeStruct((8, 128), f32)),
        in_specs=[
            pl.BlockSpec(memory_space=smem), pl.BlockSpec(memory_space=smem),
            pl.BlockSpec(memory_space=vmem), pl.BlockSpec(memory_space=pl.ANY),
        ],
        out_specs=(pl.BlockSpec(memory_space=vmem), pl.BlockSpec(memory_space=vmem)),
        scratch_shapes=[
            vmem((nz, nrow * nodes, 2 * nodes), bf16),
            vmem((2, slots + 1, tile, tile), bf16),
            vmem((2, slots + 1, tile, tile), bf16),
            vmem((2, CHUNKS, ncol, nodes, width), bf16),
            vmem((CHUNKS, nrow * nodes, width), f32),
            vmem((nodes, feats), f32),
            vmem((CHUNKS, nrow - 1, nodes, width), bf16),
            vmem((2, CHUNKS, nrow, nodes, width), bf16),
            vmem((8, width), f32),
            vmem((nrow, 8, width), f32),
            vmem((ncol, 8, width), f32),
            dma((2,)),
            dma((CHUNKS, nz)),
            dma((2, CHUNKS, ncol)),
            dma((CHUNKS, nz)),
            dma((CHUNKS, nrow - 1)),
            dma((2, CHUNKS, nrow)),
            dma((nrow,)),
            dma((nrow,)),
            dma((ncol,)),
            dma((ncol,)),
        ],
        compiler_params=pltpu.CompilerParams(collective_id=0, has_side_effects=True),
    )(prev, last, teleport, my_tiles)
    return (out[None], norms[:ITERS, 0])


def solution(mesh):
    in_specs = (
        P("col", "row", None),
        P("col", "row", None, None, None, None),
        P("col", "row", None, None),
        P("col", "row", None),
    )
    out_specs = (P("col", "row", None), P())
    body = functools.partial(local, mesh.shape["row"], mesh.shape["col"])
    return jax.shard_map(body, mesh=mesh, in_specs=in_specs, out_specs=out_specs, check_vma=False)
```

time: 515 us -> 95.8 us (0.19)
  waiting for transfers between devices: 172 us -> 0 us
  matrix products: 123 us -> 0 us
  Pallas kernels: 0 us -> 87.9 us
  local copies, waits for them, and re-layouts: 76.1 us -> 4.01 us
  loops' own time: 47.8 us -> 0 us
  blocking collectives: 39.3 us -> 0 us
  other arithmetic: 38 us -> 2.95 us
  between operations: 14.1 us -> 0.65 us
    dot_general x72 -> x0, matrix products: 123 us -> none  [the longest x24 79.4 us: source_term(): jnp.einsum('rs,sif->rif', chooser, low_part, preferred_element_type=jnp.f...]
    reduce_scatter x3 -> x0, waiting for transfers between devices: 91.2 us -> none  [local(): lax.psum_scatter(partial_value, 'row', scatter_dimension=0, tiled=True)]
    pallas_call x0 -> x1, Pallas kernels: none -> 87.9 us  [local(): pl.pallas_call(functools.partial(kernel, nrow, ncol), out_shape=(jax.Shap...]
    all_gather x3 -> x0, waiting for transfers between devices: 80.5 us -> none  [local(): lax.all_gather(rounded, 'col', axis=0, tiled=True)]
    dynamic_slice x72 -> x0, local copies, waits for them, and re-layouts: 50.8 us -> none  [the longest x48 36.7 us: accumulate(): running, _ = lax.scan(sweep, running, (blocks, offsets))]
    another operation x3 -> x0, loops' own time: 47.8 us -> none  [accumulate(): running, _ = lax.scan(sweep, running, (blocks, offsets))]
    psum x1 -> x0, blocking collectives: 39.3 us -> none  [local(): stacked = lax.psum(stacked, ('row', 'col'))]
    lt x24 -> x2, other arithmetic: 15.6 us -> 0.67 us  [the longest x1 0.66 us: local(): live = slot[None, :] < my_counts[:, None]]
  transfers between devices with their start and end apart: 6 -> 0, of which waited for: 6 -> 0; matrix products, arithmetic and copies ran while one was open for 0% -> 0% of each run, Pallas kernels for 0% -> 0%
where the time goes in v1:
time: 95.8 us; the launch traced here: 95.5 us
  Pallas kernels  87.9 us (92%)
  local copies, waits for them, and re-layouts  4.01 us (4%)
  other arithmetic  2.95 us (3%)
    pallas_call x1, Pallas kernels, local(): pl.pallas_call(functools.partial(kernel, nrow, ncol), out_shape=(jax.Shap...  87.9 us

profile of v1, /device:TPU:0, one launch (start us, length us, event | category | flops | bytes accessed | tf_op | source)
XLA Modules:
  0.0 95.5 jit_solution(16235171599046300122)
XLA Ops:
  0.6 0.7 iota_compare_fusion.2
  1.3 0.1 copy.7
  1.4 0.8 copy.6
  2.2 0.1 select_reduce_fusion
  2.3 1.0 %select_reduce_fusion.1 = s32[8,9]{0,1:T(8,128)S(1)} fusion(s32[8,9]{1,0:T(8,128)} %bitcast.9, s32[8,9]{0,1:T(8,128)S(1)} %copy.6, pred[9,9]{1,0:T(8,128)(4,1)S(1)} %iota_compare_fusion.1, pred[8,9]{1,0:T(8,128)(4,1)S(1)} %copy.7), kind=kLoop, calls=%fused_computation.2 | loop fusion | flops 3168 | bytes 1017 | tf_op jit(solution)/shard_map/reduce_max | solution.py:266
  3.3 0.1 copy.8
  3.4 0.6 compare_select_fusion.1.prev_ref
  4.0 0.6 compare_select_fusion.last_ref
  4.5 87.9 %shard_map.59 = (f32[384,256]{1,0:T(8,128)}, f32[8,128]{1,0:T(8,128)}) custom-call(s32[8,9]{1,0:T(8,128)} %compare_select_fusion.1.prev_ref, s32[8,36]{1,0:T(8,128)} %compare_select_fusion.last_ref, f32[384,256]{1,0:T(8,128)} %bitcast.7, bf16[8,9,128,128]{3,2,1,0:T(8,128)(2,1)} %bitcast.5), custom_call_target="tpu_custom_call" | custom-call | tf_op jit(solution)/shard_map/pallas_call | solution.py:274
  92.4 1.3 %slice_reduce_fusion = f32[3]{0:T(128)} fusion(f32[8,128]{1,0:T(8,128)} %get-tuple-element.5), kind=kLoop, calls=%fused_computation.8 | loop fusion | bytes 24 | tf_op jit(solution)/shard_map/slice | solution.py:307
  93.7 1.8 %copy.12 = f32[1,384,256]{2,1,0:T(8,128)} copy(f32[1,384,256]{2,1,0:T(8,128)} %bitcast.6) | data formatting | bytes 786432
  (1 shorter events, 0.0 us)

commit v2 on v1

v2 whole, which is shorter than its diff:
```python
import functools

import jax
import jax.numpy as jnp
from jax import lax
from jax.experimental import pallas as pl
from jax.experimental.pallas import tpu as pltpu
from jax.sharding import PartitionSpec as P

ITERS = 3
ALPHA = 0.1
CHUNKS = 2
PIECES = 2
MESH = pl.DeviceIdType.MESH


def kernel(
    nrow, ncol, ids_ref, counts_ref, feat_ref, tiles_ref, out_ref, norm_ref,
    table, lookup, dense, buf0, buf1, gathered, acc, current, stage, landed, squares, sq_row, sq_col,
    table_sem, tile_sem, ag_send, ag_recv, d2d_send, rs_send, rs_recv, sq_send_row, sq_recv_row, sq_send_col, sq_recv_col,
):
    nz = ncol // 2
    nodes, feats = feat_ref.shape
    slots = tiles_ref.shape[1]
    tile = tiles_ref.shape[-1]
    width = feats // CHUNKS
    row_tiles = nrow * nodes // tile
    col_tiles = nodes // tile
    places = row_tiles * col_tiles
    r = lax.axis_index("row")
    c = lax.axis_index("col")
    z = c // 2
    core = c % 2
    sibling = z * 2 + 1 - core
    bufs = (buf0, buf1)

    def tile_copy(q, slot):
        return pltpu.make_async_copy(
            tiles_ref.at[pl.ds(2 * q, 2)], bufs[slot].at[:, pl.ds(0, slots)], tile_sem.at[slot]
        )

    for slot in range(2):
        tile_copy(slot, slot).start()

    barrier = pltpu.get_barrier_semaphore()
    for k in range(1, ncol):
        pl.semaphore_signal(barrier, inc=1, device_id={"col": (c + k) % ncol}, device_id_type=MESH)
    for k in range(1, nrow):
        pl.semaphore_signal(barrier, inc=1, device_id={"row": (r + k) % nrow}, device_id_type=MESH)
    for ch in range(CHUNKS):
        cols = slice(ch * width, (ch + 1) * width)
        gathered[0, ch, c] = feat_ref[:, cols].astype(jnp.bfloat16)
    pl.semaphore_wait(barrier, ncol - 1 + nrow - 1)

    def peer(k):
        if nz == 4:
            return (z, z + 1 - 2 * (z % 2), (z + 2) % 4, 3 - z)[k]
        return (z + k) % nz

    piece = nodes // PIECES

    def block_copy(t, ch, source, target, send_sem, h):
        par = t % 2
        ref = gathered.at[par, ch, source, pl.ds(h * piece, piece)]
        return pltpu.make_async_remote_copy(
            src_ref=ref, dst_ref=ref, send_sem=send_sem, recv_sem=ag_recv.at[par, ch, source, h],
            device_id={"col": target}, device_id_type=MESH,
        )

    far = [nz == 4 and k == 3 for k in range(nz)]

    def direct(k, act):
        if far[k]:
            pl.when((z == 1) | (z == 2))(act)
        else:
            act()

    send_order = [2, 1, 3] if nz == 4 else list(range(1, nz))

    def gather_drain(ch, h):
        for k in send_order:
            def go(k=k):
                block_copy(0, ch, c, peer(k) * 2 + core, ag_send.at[ch, k, h], h).wait_send()
            direct(k, go)
        for k in range(nz):
            block_copy(0, ch, c, sibling, d2d_send.at[ch, k, h], h).wait_send()
        if nz == 4:
            @pl.when((z == 1) | (z == 2))
            def _():
                block_copy(0, ch, c, sibling, ag_send.at[ch, 0, h], h).wait_send()

    def gather_send(t, ch, h):
        if t > 0:
            gather_drain(ch, h)
        for k in send_order:
            def go(k=k):
                block_copy(t, ch, c, peer(k) * 2 + core, ag_send.at[ch, k, h], h).start()
            direct(k, go)
        block_copy(t, ch, c, sibling, d2d_send.at[ch, 0, h], h).start()

    def receive(t, ch, k):
        source = peer(k) * 2 + core
        for h in range(PIECES):
            block_copy(t, ch, source, sibling, d2d_send.at[ch, k, h], h).wait_recv()
            if nz == 4 and k == 2:
                @pl.when((z == 1) | (z == 2))
                def _():
                    block_copy(t, ch, source, 6 * (z - 1) + core, ag_send.at[ch, 0, h], h).start()
            block_copy(t, ch, source, sibling, d2d_send.at[ch, k, h], h).start()

    def share_copy(t, ch, k, h):
        par = t % 2
        span = pl.ds(h * piece, piece)
        return pltpu.make_async_remote_copy(
            src_ref=stage.at[ch, k - 1, span], dst_ref=landed.at[par, ch, r, span],
            send_sem=rs_send.at[ch, k - 1, h], recv_sem=rs_recv.at[par, ch, r, h],
            device_id={"row": (r + k) % nrow}, device_id_type=MESH,
        )

    def product(t, ch, k):
        q = peer(k)
        par = t % 2
        other = q * 2 + 1 - core
        for h in range(PIECES):
            block_copy(t, ch, other, sibling, d2d_send.at[ch, 0, h], h).wait_recv()
        source = gathered[par, ch, pl.ds(2 * q, 2)].reshape(2 * nodes, width)

        def part(rows):
            return jnp.dot(dense[q, rows], source, preferred_element_type=jnp.float32)

        if k < nz - 1:
            def one(j, carry):
                rows = pl.ds(j * nodes, nodes)
                acc[ch, rows] = part(rows) if k == 0 else acc[ch, rows] + part(rows)
                return carry
            lax.fori_loop(0, nrow, one, 0)
            return
        for h in range(PIECES):
            for k2 in range(1, nrow):
                rows = pl.ds((r + k2) % nrow * nodes + h * piece, piece)
                total = acc[ch, rows] + part(rows)
                if t > 0:
                    share_copy(t, ch, k2, h).wait_send()
                stage[ch, k2 - 1, h * piece : (h + 1) * piece] = total.astype(jnp.bfloat16)
                share_copy(t, ch, k2, h).start()
        rows = pl.ds(r * nodes, nodes)
        acc[ch, rows] = acc[ch, rows] + part(rows)

    def update(t, ch):
        par = t % 2
        cols = slice(ch * width, (ch + 1) * width)
        for h in range(PIECES):
            span = slice(h * piece, (h + 1) * piece)
            summed = acc[ch, pl.ds(r * nodes + h * piece, piece)]
            for k in range(1, nrow):
                j = (r + k) % nrow
                spot = landed.at[par, ch, j, pl.ds(h * piece, piece)]
                pltpu.make_async_remote_copy(
                    src_ref=spot, dst_ref=spot, send_sem=rs_send.at[ch, 0, h],
                    recv_sem=rs_recv.at[par, ch, j, h], device_id={"row": j}, device_id_type=MESH,
                ).wait_recv()
                summed = summed + landed[par, ch, j, span].astype(jnp.float32)
            teleport = feat_ref[span, cols]
            updated = (1.0 - ALPHA) * summed + ALPHA * teleport
            before = teleport if t == 0 else current[span, cols]
            if t < ITERS - 1:
                gathered[(t + 1) % 2, ch, c, span] = updated.astype(jnp.bfloat16)
                gather_send(t + 1, ch, h)
                current[span, cols] = updated
            else:
                out_ref[span, cols] = updated
            change = jnp.sum((updated - before) ** 2, axis=0, keepdims=True)
            squares[t : t + 1] = squares[t : t + 1] + change

    squares[...] = jnp.zeros_like(squares)
    for ch in range(CHUNKS):
        for h in range(PIECES):
            gather_send(0, ch, h)

    lane = lax.broadcasted_iota(jnp.int32, (1, table.shape[1]), 1)
    earlier = jnp.where(lane < places, slots, lane - places)

    def find(s, carry):
        ids = [ids_ref[s, k] for k in range(slots)]
        live = counts_ref[s]
        wanted = lane
        for k in range(slots):
            wanted = jnp.where(lane == places + k, ids[k], wanted)
        limit = jnp.minimum(earlier, live)
        found = jnp.full_like(lane, slots)
        for k in range(slots):
            found = jnp.where((wanted == ids[k]) & (limit > k), k, found)
        table[pl.ds(s, 1), :] = found
        return carry

    lax.fori_loop(0, ncol, find, 0)
    to_scalars = pltpu.make_async_copy(table, lookup, table_sem)
    to_scalars.start()
    zero = jnp.zeros((tile, tile), jnp.bfloat16)
    for slot in range(2):
        for half in range(2):
            bufs[slot][half, slots] = zero

    def build(step, carry):
        for slot in range(2):
            q = step * 2 + slot
            buf = bufs[slot]
            tile_copy(q, slot).wait()
            for half in range(2):
                s = 2 * q + half
                for k in range(1, slots):
                    buf[half, k] = buf[half, k] + buf[half, lookup[s, places + k]]
                for i in range(row_tiles):
                    for j in range(col_tiles):
                        at = half * nodes + j * tile
                        dense[q, i * tile : (i + 1) * tile, at : at + tile] = buf[half, lookup[s, i * col_tiles + j]]

            @pl.when(q + 2 < nz)
            def _():
                tile_copy(q + 2, slot).start()
        return carry

    to_scalars.wait()
    lax.fori_loop(0, nz // 2, build, 0)

    pending = None
    for t in range(ITERS):
        for ch in range(CHUNKS):
            for k in range(1, nz):
                if k == nz - 1 and pending is not None:
                    update(*pending)
                receive(t, ch, k)
                product(t, ch, k - 1)
            product(t, ch, nz - 1)
            pending = (t, ch)
    update(*pending)

    def sq_copy(axis, size, me, k, buffer, send, recv):
        return pltpu.make_async_remote_copy(
            src_ref=buffer.at[me], dst_ref=buffer.at[me], send_sem=send.at[k], recv_sem=recv.at[me],
            device_id={axis: (me + k) % size}, device_id_type=MESH,
        )

    total = squares[...]
    for axis, size, me, buffer, send, recv in (
        ("row", nrow, r, sq_row, sq_send_row, sq_recv_row),
        ("col", ncol, c, sq_col, sq_send_col, sq_recv_col),
    ):
        buffer[me] = total
        for k in range(1, size):
            sq_copy(axis, size, me, k, buffer, send, recv).start()
        for k in range(1, size):
            j = (me + k) % size
            pltpu.make_async_remote_copy(
                src_ref=buffer.at[me], dst_ref=buffer.at[j], send_sem=send.at[k], recv_sem=recv.at[j],
                device_id={axis: j}, device_id_type=MESH,
            ).wait_recv()
        total = buffer[0]
        for j in range(1, size):
            total = total + buffer[j]
        for k in range(1, size):
            sq_copy(axis, size, me, k, buffer, send, recv).wait_send()
    count = nrow * ncol * nodes * feats
    norms = jnp.sqrt(jnp.sum(total, axis=1, keepdims=True) / count)
    norm_ref[...] = jnp.broadcast_to(norms, norm_ref.shape)

    for ch in range(CHUNKS):
        for h in range(PIECES):
            gather_drain(ch, h)
            for k in range(1, nrow):
                share_copy(0, ch, k, h).wait_send()


def local(nrow, ncol, features, tiles, tile_ids, tile_counts):
    teleport = features[0]
    my_tiles = tiles[0, 0]
    my_ids = tile_ids[0, 0]
    my_counts = tile_counts[0, 0]
    nodes, feats = teleport.shape
    sources, slots, tile, _ = my_tiles.shape
    nz = ncol // 2
    width = feats // CHUNKS
    places = (nrow * nodes // tile) * (nodes // tile)
    lanes = pl.cdiv(places + slots, 128) * 128
    bf16, f32 = jnp.bfloat16, jnp.float32
    vmem, smem = pltpu.VMEM, pltpu.SMEM
    dma = pltpu.SemaphoreType.DMA
    out, norms = pl.pallas_call(
        functools.partial(kernel, nrow, ncol),
        out_shape=(jax.ShapeDtypeStruct((nodes, feats), f32), jax.ShapeDtypeStruct((8, 128), f32)),
        in_specs=[
            pl.BlockSpec(memory_space=smem), pl.BlockSpec(memory_space=smem),
            pl.BlockSpec(memory_space=vmem), pl.BlockSpec(memory_space=pl.ANY),
        ],
        out_specs=(pl.BlockSpec(memory_space=vmem), pl.BlockSpec(memory_space=vmem)),
        scratch_shapes=[
            vmem((ncol, lanes), jnp.int32),
            smem((ncol, lanes), jnp.int32),
            vmem((nz, nrow * nodes, 2 * nodes), bf16),
            vmem((2, slots + 1, tile, tile), bf16),
            vmem((2, slots + 1, tile, tile), bf16),
            vmem((2, CHUNKS, ncol, nodes, width), bf16),
            vmem((CHUNKS, nrow * nodes, width), f32),
            vmem((nodes, feats), f32),
            vmem((CHUNKS, nrow - 1, nodes, width), bf16),
            vmem((2, CHUNKS, nrow, nodes, width), bf16),
            vmem((8, width), f32),
            vmem((nrow, 8, width), f32),
            vmem((ncol, 8, width), f32),
            dma,
            dma((2,)),
            dma((CHUNKS, nz, PIECES)),
            dma((2, CHUNKS, ncol, PIECES)),
            dma((CHUNKS, nz, PIECES)),
            dma((CHUNKS, nrow - 1, PIECES)),
            dma((2, CHUNKS, nrow, PIECES)),
            dma((nrow,)),
            dma((nrow,)),
            dma((ncol,)),
            dma((ncol,)),
        ],
        compiler_params=pltpu.CompilerParams(collective_id=0, has_side_effects=True),
    )(my_ids, my_counts, teleport, my_tiles)
    return (out[None], norms[:ITERS, 0])


def solution(mesh):
    in_specs = (
        P("col", "row", None),
        P("col", "row", None, None, None, None),
        P("col", "row", None, None),
        P("col", "row", None),
    )
    out_specs = (P("col", "row", None), P())
    body = functools.partial(local, mesh.shape["row"], mesh.shape["col"])
    return jax.shard_map(body, mesh=mesh, in_specs=in_specs, out_specs=out_specs, check_vma=False)
```

time: 95.8 us -> 85.1 us (0.89)
  Pallas kernels: 87.9 us -> 81.2 us
  other arithmetic: 2.95 us -> 0 us
    pallas_call x1, Pallas kernels: 87.9 us -> 81.2 us  [local(): pl.pallas_call(functools.partial(kernel, nrow, ncol), out_shape=(jax.Shap...]
    select_n x2 -> x0, other arithmetic: 1.18 us -> none  [the longest x1 0.6 us: local(): prev = jnp.where(prev < 0, slots, prev)]
    reduce_max x2 -> x0, other arithmetic: 1.09 us -> none  [the longest x1 1 us: local(): prev = jnp.max(jnp.where(same, slot[None, None, :], -1), axis=2)]
where the time goes in v2:
time: 85.1 us; the launch traced here: 84.9 us
  Pallas kernels  81.2 us (95%)
  local copies, waits for them, and re-layouts  3.07 us (4%)
    pallas_call x1, Pallas kernels, local(): pl.pallas_call(functools.partial(kernel, nrow, ncol), out_shape=(jax.Shap...  81.2 us
    unnamed x1, local copies, waits for them, and re-layouts  1.77 us

profile of v2, /device:TPU:0, one launch (start us, length us, event | category | flops | bytes accessed | tf_op | source)
XLA Modules:
  0.0 84.9 jit_solution(9850330630997352222)
XLA Ops:
  0.6 81.2 %shard_map.59 = (f32[384,256]{1,0:T(8,128)}, f32[8,128]{1,0:T(8,128)}) custom-call(s32[8,9]{1,0:T(8,128)} %bitcast.8, s32[8]{0:T(128)} %bitcast.9, f32[384,256]{1,0:T(8,128)} %bitcast.6, bf16[8,9,128,128]{3,2,1,0:T(8,128)(2,1)} %bitcast.5), custom_call_target="tpu_custom_call" | custom-call | tf_op jit(solution)/shard_map/pallas_call | solution.py:288
  81.8 1.3 %slice_reduce_fusion = f32[3]{0:T(128)} fusion(f32[8,128]{1,0:T(8,128)} %get-tuple-element.5), kind=kLoop, calls=%fused_computation | loop fusion | bytes 24 | tf_op jit(solution)/shard_map/slice | solution.py:324
  83.1 1.8 %copy.7 = f32[1,384,256]{2,1,0:T(8,128)} copy(f32[1,384,256]{2,1,0:T(8,128)} %bitcast.7) | data formatting | bytes 786432
